TPU v7x, 32 devices: a whole 2x2x4 slice. The times are simulated.
32 devices in a mesh: expert: 4 (over y, core), shard: 8 (over z, x).
Axes of the slice: x: 2, y: 2, z: 4, core: 2. Of those that a mesh axis runs over, the one named last changes fastest.
Arguments:
- master_gate: float32 [128, 2048, 768], P('expert', 'shard'), may hold values from -0.125 to 0.125
- second_gate: bfloat16 [128, 2048, 768], P('expert', 'shard'), may hold values from -0.0625 to 0.0625
- master_up: float32 [128, 2048, 768], P('expert', 'shard'), may hold values from -0.125 to 0.125
- second_up: bfloat16 [128, 2048, 768], P('expert', 'shard'), may hold values from -0.0625 to 0.0625
- router_weight: float32 [2048, 128], P('shard', 'expert'), may hold values from -0.125 to 0.125
- router_gain: float32 [2048], P('shard'), may hold values from 0.25 to 1.75
Outputs:
- final_gate: bfloat16 [128, 768, 2048], P('expert', 'shard')
- final_up: bfloat16 [128, 768, 2048], P('expert', 'shard')
- serve_router: bfloat16 [2048, 128], replicated
All inputs are finite; a program needn't handle non-finite values.
Results may differ from a plain program's by a relative error of at most 0.001.
Values may be sent and summed in bfloat16 or wider, within the bound.
A program may use at most 192 MiB of HBM per device.

v0:
```python
import jax
import jax.numpy as jnp
from jax import lax
from jax.sharding import PartitionSpec as P


def per_device(master_gate, second_gate, master_up, second_up, router_weight, router_gain):
    merged_gate = master_gate + second_gate.astype(jnp.float32)
    merged_up = master_up + second_up.astype(jnp.float32)
    narrow_gate, narrow_up = (merged_gate.astype(jnp.bfloat16), merged_up.astype(jnp.bfloat16))
    final_gate, final_up = (
        lax.all_to_all(narrow_gate, "shard", split_axis=2, concat_axis=1, tiled=True),
        lax.all_to_all(narrow_up, "shard", split_axis=2, concat_axis=1, tiled=True),
    )
    final_gate = jnp.transpose(final_gate, (0, 2, 1))
    final_up = jnp.transpose(final_up, (0, 2, 1))
    part_router = (router_weight * router_gain[:, None]).astype(jnp.bfloat16)
    row_router = lax.all_gather(part_router, "shard", axis=0, tiled=True)
    serve_router = lax.all_gather(row_router, "expert", axis=1, tiled=True)
    return (final_gate, final_up, serve_router)


def solution(mesh):
    placed = (
        P("expert", "shard", None),
        P("expert", "shard", None),
        P("expert", "shard", None),
        P("expert", "shard", None),
        P("shard", "expert"),
        P("shard"),
    )
    return jax.shard_map(
        per_device,
        mesh=mesh,
        in_specs=placed,
        out_specs=(P("expert", "shard", None), P("expert", "shard", None), P()),
        check_vma=False,
    )
```

profile of v0, /device:TPU:0, one launch (start us, length us, event | category | flops | bytes accessed | tf_op | source)
XLA Modules:
  0.0 713.1 jit_solution(3689968632232905963)
XLA Ops:
  0.6 25.0 %copy.25 = f32[32,256,768]{1,0,2:T(8,128)} copy(f32[32,256,768]{2,1,0:T(8,128)} %param.6) | data formatting | bytes 50331648 | tf_op args[0]
  25.7 16.9 %copy.24 = bf16[32,256,768]{1,0,2:T(8,128)(2,1)} copy(bf16[32,256,768]{2,1,0:T(8,128)(2,1)} %param.7) | data formatting | bytes 25165824 | tf_op args[1]
  42.5 17.3 %add_convert_fusion.1 = bf16[32,256,768]{1,0,2:T(8,128)(2,1)} fusion(f32[32,256,768]{1,0,2:T(8,128)} %copy.25, bf16[32,256,768]{1,0,2:T(8,128)(2,1)} %copy.24), kind=kLoop, calls=%fused_computation.1 | loop fusion | flops 18874368 | bytes 50331648 | tf_op jit(solution)/shard_map/convert_element_type | solution.py:10
  59.8 7.3 %all-to-all-start = ((bf16[32,256,768]{1,0,2:T(8,128)(2,1)}), bf16[32,256,768]{1,0,2:T(8,128)(2,1)}, u32[]{:S(2)}, u32[]{:S(2)}) async-start(bf16[32,256,768]{1,0,2:T(8,128)(2,1)} %add_convert_fusion.1), calls=%async_computation | async-start | bytes 25165824 | tf_op jit(solution)/shard_map/all_to_all | solution.py:12
  67.1 25.0 %copy.29 = f32[32,256,768]{1,0,2:T(8,128)} copy(f32[32,256,768]{2,1,0:T(8,128)} %param.8) | data formatting | bytes 50331648 | tf_op args[2]
  92.2 16.9 %copy.28 = bf16[32,256,768]{1,0,2:T(8,128)(2,1)} copy(bf16[32,256,768]{2,1,0:T(8,128)(2,1)} %param.9) | data formatting | bytes 25165824 | tf_op args[3]
  109.0 17.3 %add_convert_fusion = bf16[32,256,768]{1,0,2:T(8,128)(2,1)} fusion(f32[32,256,768]{1,0,2:T(8,128)} %copy.29, bf16[32,256,768]{1,0,2:T(8,128)(2,1)} %copy.28), kind=kLoop, calls=%fused_computation | loop fusion | flops 18874368 | bytes 50331648 | tf_op jit(solution)/shard_map/convert_element_type | solution.py:10
  126.3 0.0 copy-start
  126.3 0.0 copy-start.1
  126.3 213.9 %all-to-all-done = bf16[32,256,768]{1,0,2:T(8,128)(2,1)} async-done(((bf16[32,256,768]{1,0,2:T(8,128)(2,1)}), bf16[32,256,768]{1,0,2:T(8,128)(2,1)}, u32[]{:S(2)}, u32[]{:S(2)}) %all-to-all-start) | async-done | bytes 12582944 | tf_op jit(solution)/shard_map/all_to_all | solution.py:12
  340.2 5.3 all-to-all-start.1
  345.5 0.0 copy-done
  345.5 0.0 copy-done.1
  345.6 292.2 %all_gather.6 = bf16[2048,32]{0,1:T(8,128)(2,1)S(1)} all-gather(bf16[256,32]{0,1:T(8,128)(2,1)S(1)} %multiply_convert_fusion), channel_id=1, replica_groups=mesh['expert'=4,'shard'=8] {'shard'}, dimensions={0}, use_global_device_ids=true | all-gather | bytes 147456 | tf_op jit(solution)/shard_map/all_gather | solution.py:18
  637.8 7.2 %all_gather.7 = bf16[2048,128]{0,1:T(8,128)(2,1)S(1)} all-gather(bf16[2048,32]{0,1:T(8,128)(2,1)S(1)} %all_gather.6), channel_id=1, replica_groups=mesh['expert'=4,'shard'=8] {'expert'}, dimensions={1}, use_global_device_ids=true | all-gather | bytes 655360 | tf_op jit(solution)/shard_map/all_gather | solution.py:19
  645.0 1.0 copy.32
  646.0 14.1 %copy.27 = bf16[32,8,256,96]{2,1,3,0:T(8,128)(2,1)} copy(bf16[32,8,256,96]{2,0,3,1:T(8,128)(2,1)} %bitcast.2) | data formatting | bytes 25165824 | tf_op jit(solution)/shard_map/all_to_all | solution.py:12
  660.0 19.5 %all_to_all.29 = bf16[32,2048,96]{1,2,0:T(8,128)(2,1)} reshape(bf16[32,8,256,96]{2,1,3,0:T(8,128)(2,1)} %copy.27) | data formatting | bytes 25165824 | tf_op jit(solution)/shard_map/all_to_all | solution.py:12
  679.5 0.0 all-to-all-done.1
  679.5 14.1 %copy.31 = bf16[32,8,256,96]{2,1,3,0:T(8,128)(2,1)} copy(bf16[32,8,256,96]{2,0,3,1:T(8,128)(2,1)} %bitcast.6) | data formatting | bytes 25165824 | tf_op jit(solution)/shard_map/all_to_all | solution.py:13
  693.6 19.5 %all_to_all.33 = bf16[32,2048,96]{1,2,0:T(8,128)(2,1)} reshape(bf16[32,8,256,96]{2,1,3,0:T(8,128)(2,1)} %copy.31) | data formatting | bytes 25165824 | tf_op jit(solution)/shard_map/all_to_all | solution.py:13
  (1 shorter events, 0.0 us)
Async XLA Ops:
  59.8 280.3 %all-to-all-start = ((bf16[32,256,768]{1,0,2:T(8,128)(2,1)}), bf16[32,256,768]{1,0,2:T(8,128)(2,1)}, u32[]{:S(2)}, u32[]{:S(2)}) async-start(bf16[32,256,768]{1,0,2:T(8,128)(2,1)} %add_convert_fusion.1), calls=%async_computation | async-start | bytes 25165824 | tf_op jit(solution)/shard_map/all_to_all | solution.py:12
  126.3 219.2 %copy-start = (f32[256,32]{0,1:T(8,128)S(1)}, f32[256,32]{0,1:T(8,128)}, u32[]{:S(2)}) copy-start(f32[256,32]{0,1:T(8,128)} %param.10) | copy-start | bytes 98308
  126.3 219.2 %copy-start.1 = (f32[256]{0:T(256)S(1)}, f32[256]{0:T(256)}, u32[]{:S(2)}) copy-start(f32[256]{0:T(256)} %param.11) | copy-start | bytes 3076
  340.2 339.3 %all-to-all-start.1 = ((bf16[32,256,768]{1,0,2:T(8,128)(2,1)}), bf16[32,256,768]{1,0,2:T(8,128)(2,1)}, u32[]{:S(2)}, u32[]{:S(2)}) async-start(bf16[32,256,768]{1,0,2:T(8,128)(2,1)} %add_convert_fusion), calls=%async_computation.1 | async-start | bytes 25165824 | tf_op jit(solution)/shard_map/all_to_all | solution.py:13
where the time goes:
time: 716 us; the launch traced here: 713 us
  blocking collectives  299 us (42%)
  waiting for transfers between devices  214 us (30%)
  local copies, waits for them, and re-layouts  152 us (21%)
  other arithmetic  34.6 us (5%)
  starting transfers between devices  12.6 us (2%)
    all_gather x1, blocking collectives, per_device(): row_router = lax.all_gather(part_router, 'shard', axis=0, tiled=True)  292 us
    all_to_all x1, waiting for transfers between devices, per_device(): lax.all_to_all(narrow_gate, 'shard', split_axis=2, concat_axis=1, tiled=T...  214 us
    unnamed x9, local copies, waits for them, and re-layouts  84.8 us
    all_to_all x2, local copies, waits for them, and re-layouts, per_device(): lax.all_to_all(narrow_up, 'shard', split_axis=2, concat_axis=1, tiled=True)  33.6 us
    all_to_all x2, local copies, waits for them, and re-layouts, per_device(): lax.all_to_all(narrow_gate, 'shard', split_axis=2, concat_axis=1, tiled=T...  33.5 us
    convert_element_type x1, other arithmetic, per_device(): merged_gate.astype(jnp.bfloat16)  17.3 us
    convert_element_type x1, other arithmetic, per_device(): merged_up.astype(jnp.bfloat16)  17.3 us
  transfers between devices with their start and end apart: 2, of which 1 were waited for; matrix products, arithmetic and copies ran while one was open for 10% of the time, Pallas kernels for 0%

commit v1 on v0

v1 whole, which is shorter than its diff:
```python
import functools

import jax
import jax.numpy as jnp
from jax import lax
from jax.experimental import pallas as pl
from jax.experimental.pallas import tpu as pltpu
from jax.sharding import PartitionSpec as P

MESH = pl.DeviceIdType.MESH
SLOTS = 3
ORDER = 0


def exchange_kernel(
    n, groups, mg, sg, mu, su, part, recv, router,
    wide, narrow, outbox, in_sem, send_sem, recv_sem, own_sem, rs_send, rs_recv, re_send, re_recv,
):
    experts, rows, _ = mg.shape
    block = outbox.shape[3]
    columns = part.shape[0]
    me = lax.axis_index("shard")
    group = lax.axis_index("expert")

    def load(e):
        slot = lax.rem(e, SLOTS)
        return (
            pltpu.make_async_copy(mg.at[e], wide.at[slot, 0], in_sem.at[slot, 0]),
            pltpu.make_async_copy(sg.at[e], narrow.at[slot, 0], in_sem.at[slot, 1]),
            pltpu.make_async_copy(mu.at[e], wide.at[slot, 1], in_sem.at[slot, 2]),
            pltpu.make_async_copy(su.at[e], narrow.at[slot, 1], in_sem.at[slot, 3]),
        )

    for e in range(SLOTS):
        for copy in load(e):
            copy.start()

    barrier = pltpu.get_barrier_semaphore()
    for j in range(1, n):
        pl.semaphore_signal(barrier, inc=1, device_id=(group, lax.rem(me + j, n)), device_id_type=MESH)
    for j in range(1, groups):
        pl.semaphore_signal(barrier, inc=1, device_id=(lax.rem(group + j, groups), me), device_id_type=MESH)
    pl.semaphore_wait(barrier, n - 1 + groups - 1)

    band = router.at[pl.ds(pl.multiple_of(group * columns, columns), columns)]
    spot = band.at[:, pl.ds(pl.multiple_of(me * rows, rows), rows)]
    own_router = pltpu.make_async_copy(part, spot, own_sem.at[1])
    own_router.start()
    router_rows = []
    for j in range(1, n):
        router_rows.append(
            pltpu.make_async_remote_copy(
                src_ref=part, dst_ref=spot, send_sem=rs_send.at[j], recv_sem=rs_recv.at[j],
                device_id=(group, lax.rem(me + j, n)), device_id_type=MESH,
            )
        )
        router_rows[-1].start()

    half, quarter = n // 2, max(n // 4, 1)
    lower = me < half
    outer = jnp.logical_or(me < quarter, me >= n - quarter)
    near = [lax.rem(me + j, half) + jnp.where(lower, 0, half) for j in range(1, half)]
    far = [lax.rem(me + j, half) + jnp.where(lower, half, 0) for j in range(half)]

    def send(e, peer):
        pltpu.make_async_remote_copy(
            src_ref=outbox.at[peer, e], dst_ref=recv.at[me, e],
            send_sem=send_sem.at[peer], recv_sem=recv_sem.at[me],
            device_id=(group, peer), device_id_type=MESH,
        ).start()

    def send_first(e):
        if ORDER == 0:
            for peer in far + near:
                send(e, peer)
        elif ORDER == 1:
            for peer in near + far:
                send(e, peer)
        else:
            @pl.when(outer)
            def _():
                for peer in near:
                    send(e, peer)

            @pl.when(jnp.logical_not(outer))
            def _():
                for peer in far:
                    send(e, peer)

    def send_second(e):
        @pl.when(outer)
        def _():
            for peer in far:
                send(e, peer)

        @pl.when(jnp.logical_not(outer))
        def _():
            for peer in near:
                send(e, peer)

    def step(e, _):
        slot = lax.rem(e, SLOTS)
        for copy in load(e):
            copy.wait()
        for which in range(2):
            merged = wide[slot, which] + narrow[slot, which].astype(jnp.float32)
            turned = merged.astype(jnp.bfloat16).T
            for d in range(n):
                outbox[d, e, which] = turned[d * block:(d + 1) * block]

        @pl.when(e + SLOTS < experts)
        def _():
            for copy in load(e + SLOTS):
                copy.start()

        @pl.when(e > 0)
        def _():
            send_first(e - 1)

        return 0

    lax.fori_loop(0, experts, step, 0)
    send_first(experts - 1)
    if ORDER == 2:
        lax.fori_loop(0, experts, lambda e, c: (send_second(e), c)[1], 0)

    own = pltpu.make_async_copy(outbox.at[me], recv.at[me], own_sem.at[0])
    own.start()

    own_router.wait()
    for copy in router_rows:
        copy.wait()
    router_bands = []
    for j in range(1, groups):
        router_bands.append(
            pltpu.make_async_remote_copy(
                src_ref=band, dst_ref=band, send_sem=re_send.at[j], recv_sem=re_recv.at[j],
                device_id=(lax.rem(group + j, groups), me), device_id_type=MESH,
            )
        )
        router_bands[-1].start()
    for copy in router_bands:
        copy.wait()

    own.wait()
    for j in range(1, n):
        peer = lax.rem(me + j, n)
        pltpu.make_async_copy(outbox.at[peer], outbox.at[peer], send_sem.at[peer]).wait()
        pltpu.make_async_copy(recv.at[peer], recv.at[peer], recv_sem.at[peer]).wait()


def interleave_kernel(n, recv, gate, up):
    rows = recv.shape[-1]
    for d in range(n):
        gate[:, :, d * rows:(d + 1) * rows] = recv[d, :, 0]
        up[:, :, d * rows:(d + 1) * rows] = recv[d, :, 1]


def by_kernel(n, groups, master_gate, second_gate, master_up, second_up, part):
    experts, rows, width = master_gate.shape
    block = width // n
    columns = part.shape[0]
    anywhere = pl.BlockSpec(memory_space=pl.ANY)
    dma = pltpu.SemaphoreType.DMA
    recv, router = pl.pallas_call(
        functools.partial(exchange_kernel, n, groups),
        out_shape=(
            jax.ShapeDtypeStruct((n, experts, 2, block, rows), jnp.bfloat16),
            jax.ShapeDtypeStruct((groups * columns, n * rows), jnp.bfloat16),
        ),
        in_specs=[anywhere] * 5,
        out_specs=(anywhere, anywhere),
        scratch_shapes=[
            pltpu.VMEM((SLOTS, 2, rows, width), jnp.float32),
            pltpu.VMEM((SLOTS, 2, rows, width), jnp.bfloat16),
            pltpu.VMEM((n, experts, 2, block, rows), jnp.bfloat16),
            dma((SLOTS, 4)), dma((n,)), dma((n,)), dma((2,)),
            dma((n,)), dma((n,)), dma((groups,)), dma((groups,)),
        ],
        compiler_params=pltpu.CompilerParams(collective_id=0, has_side_effects=True),
    )(master_gate, second_gate, master_up, second_up, part)
    some = 2 if experts % 2 == 0 else 1
    whole = jax.ShapeDtypeStruct((experts, block, n * rows), jnp.bfloat16)
    gate, up = pl.pallas_call(
        functools.partial(interleave_kernel, n),
        grid=(experts // some,),
        out_shape=(whole, whole),
        in_specs=[pl.BlockSpec((n, some, 2, block, rows), lambda i: (0, i, 0, 0, 0))],
        out_specs=(pl.BlockSpec((some, block, n * rows), lambda i: (i, 0, 0)),) * 2,
    )(recv)
    return gate, up, router.T


def by_collectives(master_gate, second_gate, master_up, second_up, part):
    def moved(master, second):
        narrow = (master + second.astype(jnp.float32)).astype(jnp.bfloat16)
        sent = lax.all_to_all(narrow, "shard", split_axis=2, concat_axis=1, tiled=True)
        return jnp.transpose(sent, (0, 2, 1))

    bands = lax.all_gather(part.T, "shard", axis=0, tiled=True)
    router = lax.all_gather(bands, "expert", axis=1, tiled=True)
    return moved(master_gate, second_gate), moved(master_up, second_up), router


def per_device(n, groups, master_gate, second_gate, master_up, second_up, router_weight, router_gain):
    part = (router_weight * router_gain[:, None]).astype(jnp.bfloat16).T
    experts, rows, width = master_gate.shape
    fits = n >= 4 and n % 4 == 0 and groups > 1 and rows % 128 == 0 and width % (16 * n) == 0
    fits = fits and part.shape[0] % 16 == 0 and experts > SLOTS
    fits = fits and experts * rows * width * 4 + SLOTS * rows * width * 12 < 40 * 2**20
    if fits:
        return by_kernel(n, groups, master_gate, second_gate, master_up, second_up, part)
    return by_collectives(master_gate, second_gate, master_up, second_up, part)


def solution(mesh):
    placed = (
        P("expert", "shard", None),
        P("expert", "shard", None),
        P("expert", "shard", None),
        P("expert", "shard", None),
        P("shard", "expert"),
        P("shard"),
    )
    return jax.shard_map(
        functools.partial(per_device, mesh.shape["shard"], mesh.shape["expert"]),
        mesh=mesh,
        in_specs=placed,
        out_specs=(P("expert", "shard", None), P("expert", "shard", None), P()),
        check_vma=False,
    )
```

time: 716 us -> 581 us (0.81)
  Pallas kernels: 0 us -> 576 us
  blocking collectives: 299 us -> 0 us
  waiting for transfers between devices: 214 us -> 0 us
  local copies, waits for them, and re-layouts: 152 us -> 2.04 us
  other arithmetic: 34.6 us -> 1.37 us
  starting transfers between devices: 12.6 us -> 0 us
    pallas_call x0 -> x2, Pallas kernels: none -> 576 us  [the longest x1 553 us: by_kernel(): pl.pallas_call(functools.partial(exchange_kernel, n, groups), out_shape=(...]
    all_gather x2 -> x0, blocking collectives: 299 us -> none  [the longest x1 292 us: per_device(): row_router = lax.all_gather(part_router, 'shard', axis=0, tiled=True)]
    all_to_all x2 -> x0, waiting for transfers between devices: 214 us -> none  [the longest x1 214 us: per_device(): lax.all_to_all(narrow_gate, 'shard', split_axis=2, concat_axis=1, tiled=T...]
    unnamed x9 -> x1, local copies, waits for them, and re-layouts: 84.8 us -> 2.04 us
    all_to_all x4 -> x0, local copies, waits for them, and re-layouts: 67.1 us -> none  [the longest x2 33.6 us: per_device(): lax.all_to_all(narrow_up, 'shard', split_axis=2, concat_axis=1, tiled=True)]
    convert_element_type x3 -> x0, other arithmetic: 34.6 us -> none  [the longest x1 17.3 us: per_device(): merged_gate.astype(jnp.bfloat16)]
    all_to_all x2 -> x0, starting transfers between devices: 12.6 us -> none  [the longest x1 7.28 us: per_device(): lax.all_to_all(narrow_gate, 'shard', split_axis=2, concat_axis=1, tiled=T...]
  transfers between devices with their start and end apart: 2 -> 0, of which waited for: 1 -> 0; matrix products, arithmetic and copies ran while one was open for 10% -> 0% of each run, Pallas kernels for 0% -> 0%
where the time goes in v1:
time: 581 us; the launch traced here: 580 us
  Pallas kernels  576 us (99%)
    pallas_call x1, Pallas kernels, by_kernel(): pl.pallas_call(functools.partial(exchange_kernel, n, groups), out_shape=(...  553 us
    pallas_call x1, Pallas kernels, by_kernel(): pl.pallas_call(functools.partial(interleave_kernel, n), grid=(experts //...  22.9 us

profile of v1, /device:TPU:0, one launch (start us, length us, event | category | flops | bytes accessed | tf_op | source)
XLA Modules:
  0.0 580.3 jit_solution(2706692291963753589)
XLA Ops:
  0.6 1.4 fusion.part
  2.0 553.3 %shard_map.85 = (bf16[8,32,2,96,256]{4,3,2,1,0:T(8,128)(2,1)}, bf16[128,2048]{1,0:T(8,128)(2,1)}) custom-call(f32[32,256,768]{2,1,0:T(8,128)} %mg.1, bf16[32,256,768]{2,1,0:T(8,128)(2,1)} %sg.1, f32[32,256,768]{2,1,0:T(8,128)} %mu.1, bf16[32,256,768]{2,1,0:T(8,128)(2,1)} %su.1, bf16[32,256]{1,0:T(8,128)(2,1)} %fusion.part), custom_call_target="tpu_custom_call" | custom-call | tf_op jit(solution)/shard_map/pallas_call | solution.py:165
  555.3 2.0 copy.9
  557.4 22.9 %shard_map.86 = (bf16[32,96,2048]{2,1,0:T(8,128)(2,1)}, bf16[32,96,2048]{2,1,0:T(8,128)(2,1)}) custom-call(bf16[8,32,2,96,256]{4,3,2,1,0:T(8,128)(2,1)} %get-tuple-element.7.recv), custom_call_target="tpu_custom_call" | custom-call | tf_op jit(solution)/shard_map/pallas_call | solution.py:184
